TPU v7x, 256 devices: a whole 4x4x8 slice. The times are simulated.
256 devices in a mesh: kx: 16 (over z, x_lo), ky: 4 (over x_hi, core), kz: 4 (over y).
Axes of the slice: x: 4 (x_hi: 2, x_lo: 2; x = x_hi * 2 + x_lo), y: 4, z: 8, core: 2. Of those that a mesh axis runs over, the one named last changes fastest.
Arguments:
- coefficients: bfloat16 [2, 16, 4, 4, 512, 2048], P(None, 'kx', 'ky', 'kz'), may hold values from -1 to 1
- shift_blocks: int32 [3], replicated, may hold values from 1 to 15, as said below
Outputs:
- centre: float32 [3, 512], replicated
- spread: float32 [3, 512], replicated
- coherence: float32 [3, 16, 4, 4], P(None, 'kx', 'ky', 'kz')
Inputs may be any that keep to these rules, and one draw needn't show every extreme that they name: The coefficients one period further along direction d are those of the first k-point of the string with plane-wave index g read at (g + 128 * shift_blocks[d]) mod 2048.
All inputs are finite; a program needn't handle non-finite values.
Results may differ from a plain program's by a relative error of at most 0.0003.
Values may be sent and summed in bfloat16 or wider, within the bound.
A program may use at most 128 MiB of HBM per device.

v0:
```python
import jax
import jax.numpy as jnp
from jax import lax
from jax.sharding import Mesh
from jax.sharding import PartitionSpec as P

KX = ("kx_0", "kx_1")
KY = ("ky_0", "ky_1")
KX_KY_KZ = ("kx_0", "kx_1", "ky_0", "ky_1", "kz")


def passed_along(value, axis, steps):
    count = lax.axis_size(axis)
    pairs = [(source, (source + steps) % count) for source in range(count)]
    return lax.ppermute(value, axis, pairs)


def one_axis_at_a_time(array, axes):
    for axis in axes:
        array = lax.psum(array, axis)
    return array


def pair_measure(own_point, partner):
    bands = own_point.shape[1]
    left_side = jnp.concatenate([own_point[0], own_point[1]], axis=1)
    right_side = jnp.concatenate(
        [
            jnp.concatenate([partner[0], partner[1]], axis=1),
            jnp.concatenate([partner[1], -partner[0]], axis=1),
        ],
        axis=0,
    )
    product = lax.dot_general(
        left_side, right_side, (((1,), (1,)), ((), ())), preferred_element_type=jnp.float32
    )
    real_part = product[:, :bands]
    imag_part = product[:, bands:]
    phases = jnp.arctan2(jnp.diagonal(imag_part), jnp.diagonal(real_part))
    coherence = jnp.sum(real_part * real_part + imag_part * imag_part) / bands
    return (phases, coherence)


def shards(coefficients, shift_blocks):
    planes = coefficients.shape[1]
    bands = coefficients.shape[4]
    width = coefficients.shape[5]
    own_planes = coefficients.reshape(2, planes, bands, width)
    shifts = shift_blocks * 128
    measure = jax.vmap(pair_measure, in_axes=(1, 1))
    next_first = passed_along(own_planes[:, 0], KX, -1)
    x_wrap = lax.axis_index(KX) == lax.axis_size(KX) - 1
    next_first = jnp.where(x_wrap, jnp.roll(next_first, -shifts[0], axis=-1), next_first)
    x_partner = jnp.concatenate([own_planes[:, 1:], next_first[:, None]], axis=1)
    x_phases, x_coherence = measure(own_planes, x_partner)
    earlier = passed_along(own_planes, KY, 1)
    y_wrap = lax.axis_index(KY) == 0
    y_partner = jnp.where(y_wrap, jnp.roll(own_planes, -shifts[1], axis=-1), own_planes)
    y_phases, y_earlier = measure(earlier, y_partner)
    y_coherence = passed_along(y_earlier, KY, -1)
    z_later = passed_along(own_planes, "kz", -1)
    z_wrap = lax.axis_index("kz") == lax.axis_size("kz") - 1
    z_partner = jnp.where(z_wrap, jnp.roll(z_later, -shifts[2], axis=-1), z_later)
    z_phases, z_coherence = measure(own_planes, z_partner)
    phases = jnp.stack([x_phases, y_phases, z_phases])
    coherence = jnp.stack([x_coherence, y_coherence, z_coherence]).reshape(3, planes, 1, 1)
    k_total = planes * lax.axis_size(KX) * lax.axis_size(KY) * lax.axis_size("kz")
    counts = jnp.array(
        [planes * lax.axis_size(KX), lax.axis_size(KY), lax.axis_size("kz")], jnp.float32
    )
    phase_sum = jnp.sum(phases, axis=1)
    totals, squares = (
        one_axis_at_a_time(phase_sum, KX_KY_KZ),
        one_axis_at_a_time(jnp.sum(phases * phases, axis=1), KX_KY_KZ),
    )
    mean_phase = totals / k_total
    variance = squares / k_total - mean_phase * mean_phase
    centre = -counts[:, None] * mean_phase / (2.0 * jnp.pi)
    spread = (counts[:, None] / (2.0 * jnp.pi)) ** 2 * variance
    return (centre, spread, coherence)


def solution(mesh):
    split = Mesh(
        mesh.devices.reshape(8, 2, 2, 2, mesh.shape["kz"]), ("kx_0", "kx_1", "ky_0", "ky_1", "kz")
    )
    in_specs = (P(None, KX, KY, "kz", None, None), P())
    out_specs = (P(), P(), P(None, KX, KY, "kz"))
    return jax.shard_map(
        shards, mesh=split, in_specs=in_specs, out_specs=out_specs, check_vma=False
    )
```

profile of v0, /device:TPU:2, one launch (start us, length us, event | category | flops | bytes accessed | tf_op | source)
XLA Modules:
  0.0 270.2 jit_solution(11188901696247821564)
XLA Ops:
  0.6 3.1 %collective-permute-start.2 = (bf16[2,1,512,2048]{3,2,0,1:T(8,128)(2,1)}, bf16[2,1,512,2048]{3,2,0,1:T(8,128)(2,1)}, u32[]{:S(2)}, u32[]{:S(2)}) collective-permute-start(bf16[2,1,512,2048]{3,2,0,1:T(8,128)(2,1)} %bitcast.97), channel_id=1, source_target_pairs={{0,3},{1,0},{2,1},{3,2},{4,7},{5,4},{6,5},{7,6},{8,11},{9,8},{10,9... | collective-permute-start | bytes 12582920 | tf_op jit(solution)/shard_map/ppermute | solution.py:15
  8.2 6.5 %fusion.39 = bf16[2,1,512,2048]{3,2,1,0:T(8,128)(2,1)S(1)} fusion(bf16[2,1,512,2048]{3,2,0,1:T(8,128)(2,1)} %bitcast.100, s32[]{:T(128)S(6)} %select_n.67, pred[]{:T(512)S(6)} %eq.14), kind=kLoop, calls=%fused_computation.81 | loop fusion | flops 10485760 | bytes 8388613 | tf_op jit(solution)/shard_map/jit(_where)/select_n | solution.py:58
  14.7 1.5 fusion.35
  16.2 1.6 slice_bitcast_fusion.3
  18.3 4.2 %fusion.24 = bf16[2,1,512,2048]{3,2,0,1:T(8,128)(2,1)S(1)} fusion(bf16[2,1,512,2048]{3,2,0,1:T(8,128)(2,1)S(1)} %bitcast.101, s32[]{:T(128)S(6)} %select_n.67, pred[]{:T(512)S(6)} %eq.14), kind=kLoop, calls=%fused_computation.39 | loop fusion | flops 10485760 | bytes 8388613 | tf_op jit(solution)/shard_map/jit(_where)/select_n | solution.py:58
  22.5 1.5 slice_bitcast_fusion.2
  24.1 2.5 slice_bitcast_fusion.7
  26.5 67.3 %collective-permute-done.2 = bf16[2,1,512,2048]{3,2,0,1:T(8,128)(2,1)} collective-permute-done((bf16[2,1,512,2048]{3,2,0,1:T(8,128)(2,1)}, bf16[2,1,512,2048]{3,2,0,1:T(8,128)(2,1)}, u32[]{:S(2)}, u32[]{:S(2)}) %collective-permute-start.2) | collective-permute-done | bytes 4194336 | tf_op jit(solution)/shard_map/ppermute | solution.py:15
  93.9 7.8 %fusion.40 = bf16[2,1,512,2048]{3,2,1,0:T(8,128)(2,1)S(1)} fusion(bf16[2,1,512,2048]{3,2,0,1:T(8,128)(2,1)} %collective-permute-done.2, s32[]{:T(128)S(6)} %select_n.69, pred[]{:T(512)S(6)} %eq.15), kind=kLoop, calls=%fused_computation.82 | loop fusion | flops 10485760 | bytes 8388613 | tf_op jit(solution)/shard_map/jit(_where)/select_n | solution.py:63
  102.0 8.0 %fusion.22 = bf16[2,1,512,2048]{3,2,0,1:T(8,128)(2,1)S(1)} fusion(bf16[2,1,512,2048]{3,2,0,1:T(8,128)(2,1)} %collective-permute-done.2, s32[]{:T(128)S(6)} %select_n.69, pred[]{:T(512)S(6)} %eq.15), kind=kLoop, calls=%fused_computation.37 | loop fusion | flops 10485760 | bytes 8388613 | tf_op jit(solution)/shard_map/jit(_where)/select_n | solution.py:63
  110.1 8.2 %fusion.29 = f32[1,512,1024]{2,1,0:T(8,128)} fusion(bf16[1,512,2048]{2,1,0:T(8,128)(2,1)S(1)} %fusion.36, bf16[1,512,2048]{2,1,0:T(8,128)(2,1)S(1)} %slice_bitcast_fusion, bf16[1,512,2048]{2,1,0:T(8,128)(2,1)S(1)} %slice_bitcast_fusion.1, bf16[1,512,2048]{2,1,0:T(8,128)(2,1)} %get-tuple-element.18, bf16[1,512,2048]{2,1,0:T(8,128)(2,1)} %get-tuple-element.17), kind=kOutput, calls=%fused_computation.54 | convolution fusion | flops 4336910336 | bytes 12582912 | tf_op jit(solution)/shard_map/vmap()/dot_general | solution.py:34
  118.3 2.5 add_reduce_fusion
  120.8 4.5 %gather_fusion.4 = f32[512]{0:T(512)S(1)} fusion(f32[512,512]{1,0:T(8,128)S(1)} %get-tuple-element.27, s32[512]{0:T(512)S(1)} %bitcast.91), kind=kCustom, calls=%fused_computation.4 | custom fusion | bytes 8192 | tf_op jit(solution)/shard_map/vmap(jit(diagonal))/cond/branch_0_fun/gather | solution.py:39
  125.3 4.5 %gather_fusion.5 = f32[512]{0:T(512)S(1)} fusion(f32[512,512]{1,0:T(8,128)S(1)} %get-tuple-element.26, s32[512]{0:T(512)S(1)} %bitcast.92), kind=kCustom, calls=%fused_computation.5 | custom fusion | bytes 8192 | tf_op jit(solution)/shard_map/vmap(jit(diagonal))/cond/branch_0_fun/gather | solution.py:39
  129.9 3.3 %slice_bitcast_fusion.5 = bf16[1,512,2048]{2,1,0:T(8,128)(2,1)} fusion(bf16[2,1,512,2048]{3,2,1,0:T(8,128)(2,1)} %bitcast.12), kind=kLoop, calls=%fused_computation.51 | loop fusion | bytes 4194304 | tf_op jit(solution)/shard_map/vmap()/squeeze;vmap()/transpose | solution.py:26
  133.2 3.2 %slice_bitcast_fusion.4 = bf16[1,512,2048]{2,1,0:T(8,128)(2,1)} fusion(bf16[2,1,512,2048]{3,2,0,1:T(8,128)(2,1)} %collective-permute-done.1), kind=kLoop, calls=%fused_computation.50 | loop fusion | bytes 4194304 | tf_op jit(solution)/shard_map/vmap()/squeeze;vmap()/transpose | solution.py:26
  136.4 8.1 %fusion.30 = f32[1,512,1024]{2,1,0:T(8,128)} fusion(bf16[1,512,2048]{2,1,0:T(8,128)(2,1)S(1)} %copy-done.1, bf16[1,512,2048]{2,1,0:T(8,128)(2,1)S(1)} %copy-done.3, bf16[1,512,2048]{2,1,0:T(8,128)(2,1)S(1)} %copy-done.2, bf16[1,512,2048]{2,1,0:T(8,128)(2,1)} %slice_bitcast_fusion.4, bf16[1,512,2048]{2,1,0:T(8,128)(2,1)} %slice_bitcast_fusion.5), kind=kOutput, calls=%fused_computation.55 | convolution fusion | flops 4336910336 | bytes 12582912 | tf_op jit(solution)/shard_map/vmap()/dot_general | solution.py:34
  144.5 2.5 add_reduce_fusion.1
  147.0 4.5 %gather_fusion.2 = f32[512]{0:T(512)S(1)} fusion(f32[512,512]{1,0:T(8,128)S(1)} %get-tuple-element.24, s32[512]{0:T(512)S(1)} %bitcast.93), kind=kCustom, calls=%fused_computation.2 | custom fusion | bytes 8192 | tf_op jit(solution)/shard_map/vmap(jit(diagonal))/cond/branch_0_fun/gather | solution.py:39
  151.5 4.5 %gather_fusion.3 = f32[512]{0:T(512)S(1)} fusion(f32[512,512]{1,0:T(8,128)S(1)} %get-tuple-element.23, s32[512]{0:T(512)S(1)} %bitcast.94), kind=kCustom, calls=%fused_computation.3 | custom fusion | bytes 8192 | tf_op jit(solution)/shard_map/vmap(jit(diagonal))/cond/branch_0_fun/gather | solution.py:39
  156.1 6.7 %fusion.26 = bf16[2,512,2048]{2,1,0:T(8,128)(2,1)S(1)} fusion(bf16[2,512,2048]{2,1,0:T(8,128)(2,1)} %collective-permute-done, s32[]{:T(128)S(6)} %select_n.58, pred[]{:T(512)S(6)} %eq.13), kind=kLoop, calls=%fused_computation.41 | loop fusion | flops 10485760 | bytes 8388613 | tf_op jit(solution)/shard_map/jit(_where)/select_n | solution.py:53
  163.2 8.1 %fusion.31 = f32[1,512,1024]{2,1,0:T(8,128)} fusion(bf16[1,512,2048]{2,1,0:T(8,128)(2,1)S(1)} %get-tuple-element.15, bf16[1,512,2048]{2,1,0:T(8,128)(2,1)S(1)} %get-tuple-element.16, bf16[1,512,2048]{2,1,0:T(8,128)(2,1)S(1)} %get-tuple-element.14, bf16[1,512,2048]{2,1,0:T(8,128)(2,1)} %get-tuple-element.18, bf16[1,512,2048]{2,1,0:T(8,128)(2,1)} %get-tuple-element.17), kind=kOutput, calls=%fused_computation.56 | convolution fusion | flops 4336910336 | bytes 12582912 | tf_op jit(solution)/shard_map/vmap()/dot_general | solution.py:34
  171.3 2.5 add_reduce_fusion.2
  173.8 4.5 %gather_fusion = f32[512]{0:T(512)S(1)} fusion(f32[512,512]{1,0:T(8,128)S(1)} %get-tuple-element.21, s32[512]{0:T(512)S(1)} %bitcast.95), kind=kCustom, calls=%fused_computation | custom fusion | bytes 8192 | tf_op jit(solution)/shard_map/vmap(jit(diagonal))/cond/branch_0_fun/gather | solution.py:39
  178.4 4.5 %gather_fusion.1 = f32[512]{0:T(512)S(1)} fusion(f32[512,512]{1,0:T(8,128)S(1)} %get-tuple-element.20, s32[512]{0:T(512)S(1)} %bitcast.96), kind=kCustom, calls=%fused_computation.1 | custom fusion | bytes 8192 | tf_op jit(solution)/shard_map/vmap(jit(diagonal))/cond/branch_0_fun/gather | solution.py:39
  184.2 2.1 collective-permute-start.3
  187.1 32.8 %all-reduce = (f32[3,512]{1,0:T(4,128)S(1)}, f32[3,512]{1,0:T(4,128)S(1)}) all-reduce(f32[3,512]{1,0:T(4,128)S(1)} %maximum_bitcast_fusion.23, f32[3,512]{1,0:T(4,128)S(1)} %maximum_multiply_fusion), channel_id=1, replica_groups=mesh['kx_0'=8,'kx_1'=2,'ky_0'=2,'ky_1'=2,'kz'=4] {'kx_0'}, use_global_device_ids=true, to_apply=%region_0.2 | all-reduce | flops 3072 | bytes 24576 | tf_op jit(solution)/shard_map/psum | solution.py:20
  219.8 19.9 %all-reduce.4 = (f32[3,512]{1,0:T(4,128)S(1)}, f32[3,512]{1,0:T(4,128)S(1)}) all-reduce(f32[3,512]{1,0:T(4,128)S(1)} %get-tuple-element.4, f32[3,512]{1,0:T(4,128)S(1)} %get-tuple-element.5), channel_id=1, replica_groups=mesh['kx_0'=8,'kx_1'=2,'ky_0'=2,'ky_1'=2,'kz'=4] {'kx_1'}, use_global_device_ids=true, to_apply=%region_1.3 | all-reduce | flops 3072 | bytes 24576 | tf_op jit(solution)/shard_map/psum | solution.py:20
  239.7 10.5 %all-reduce.3 = (f32[3,512]{1,0:T(4,128)S(1)}, f32[3,512]{1,0:T(4,128)S(1)}) all-reduce(f32[3,512]{1,0:T(4,128)S(1)} %get-tuple-element.12, f32[3,512]{1,0:T(4,128)S(1)} %get-tuple-element.13), channel_id=1, replica_groups=mesh['kx_0'=8,'kx_1'=2,'ky_0'=2,'ky_1'=2,'kz'=4] {'ky_0'}, use_global_device_ids=true, to_apply=%region_2.4 | all-reduce | flops 3072 | bytes 24576 | tf_op jit(solution)/shard_map/psum | solution.py:20
  250.2 3.3 %all-reduce.2 = (f32[3,512]{1,0:T(4,128)S(1)}, f32[3,512]{1,0:T(4,128)S(1)}) all-reduce(f32[3,512]{1,0:T(4,128)S(1)} %get-tuple-element.10, f32[3,512]{1,0:T(4,128)S(1)} %get-tuple-element.11), channel_id=1, replica_groups=mesh['kx_0'=8,'kx_1'=2,'ky_0'=2,'ky_1'=2,'kz'=4] {'ky_1'}, use_global_device_ids=true, to_apply=%region_3.5 | all-reduce | flops 3072 | bytes 24576 | tf_op jit(solution)/shard_map/psum | solution.py:20
  253.5 14.9 %all-reduce.1 = (f32[3,512]{1,0:T(4,128)S(1)}, f32[3,512]{1,0:T(4,128)S(1)}) all-reduce(f32[3,512]{1,0:T(4,128)S(1)} %get-tuple-element.8, f32[3,512]{1,0:T(4,128)S(1)} %get-tuple-element.9), channel_id=1, replica_groups=mesh['kx_0'=8,'kx_1'=2,'ky_0'=2,'ky_1'=2,'kz'=4] {'kz'}, use_global_device_ids=true, to_apply=%region_4.6 | all-reduce | flops 3072 | bytes 24576 | tf_op jit(solution)/shard_map/psum | solution.py:20
  269.1 1.1 maximum_bitcast_fusion.24
  (30 shorter events, 4.0 us)
Async XLA Ops:
  0.6 93.2 %collective-permute-start.2 = (bf16[2,1,512,2048]{3,2,0,1:T(8,128)(2,1)}, bf16[2,1,512,2048]{3,2,0,1:T(8,128)(2,1)}, u32[]{:S(2)}, u32[]{:S(2)}) collective-permute-start(bf16[2,1,512,2048]{3,2,0,1:T(8,128)(2,1)} %bitcast.97), channel_id=1, source_target_pairs={{0,3},{1,0},{2,1},{3,2},{4,7},{5,4},{6,5},{7,6},{8,11},{9,8},{10,9... | collective-permute-start | bytes 12582920 | tf_op jit(solution)/shard_map/ppermute | solution.py:15
  3.7 126.1 %collective-permute-start.1 = (bf16[2,1,512,2048]{3,2,0,1:T(8,128)(2,1)}, bf16[2,1,512,2048]{3,2,0,1:T(8,128)(2,1)}, u32[]{:S(2)}, u32[]{:S(2)}) collective-permute-start(bf16[2,1,512,2048]{3,2,0,1:T(8,128)(2,1)} %bitcast.98), channel_id=1, source_target_pairs={{0,4},{4,8},{8,12},{12,0},{1,5},{5,9},{9,13},{13,1},{2,6},{6,10},{... | collective-permute-start | bytes 12582920 | tf_op jit(solution)/shard_map/ppermute | solution.py:15
  3.7 152.3 %collective-permute-start = (bf16[2,512,2048]{2,1,0:T(8,128)(2,1)}, bf16[2,512,2048]{2,1,0:T(8,128)(2,1)}, u32[]{:S(2)}, u32[]{:S(2)}) collective-permute-start(bf16[2,512,2048]{2,1,0:T(8,128)(2,1)} %bitcast.99), channel_id=1, source_target_pairs={{0,240},{16,0},{32,16},{48,32},{64,48},{80,64},{96,80},{112,96},{1... | collective-permute-start | bytes 12582920 | tf_op jit(solution)/shard_map/ppermute | solution.py:15
  14.7 3.6 %copy-start = (bf16[2,1,1,1,512,2048]{5,4,3,2,1,0:T(8,128)(2,1)S(1)}, bf16[2,1,1,1,512,2048]{5,4,3,2,1,0:T(8,128)(2,1)}, u32[]{:S(2)}) copy-start(bf16[2,1,1,1,512,2048]{5,4,3,2,1,0:T(8,128)(2,1)} %param.5) | copy-start | bytes 12582916
  129.9 6.6 %copy-start.1 = (bf16[1,512,2048]{2,1,0:T(8,128)(2,1)S(1)}, bf16[1,512,2048]{2,1,0:T(8,128)(2,1)}, u32[]{:S(2)}) copy-start(bf16[1,512,2048]{2,1,0:T(8,128)(2,1)} %fusion.35) | copy-start | bytes 6291460
  129.9 6.5 %copy-start.2 = (bf16[1,512,2048]{2,1,0:T(8,128)(2,1)S(1)}, bf16[1,512,2048]{2,1,0:T(8,128)(2,1)}, u32[]{:S(2)}) copy-start(bf16[1,512,2048]{2,1,0:T(8,128)(2,1)} %slice_bitcast_fusion.3) | copy-start | bytes 6291460
  129.9 6.5 %copy-start.3 = (bf16[1,512,2048]{2,1,0:T(8,128)(2,1)S(1)}, bf16[1,512,2048]{2,1,0:T(8,128)(2,1)}, u32[]{:S(2)}) copy-start(bf16[1,512,2048]{2,1,0:T(8,128)(2,1)} %slice_bitcast_fusion.2) | copy-start | bytes 6291460
  171.3 97.1 %copy-start.4 = (f32[3]{0:T(128)S(1)}, f32[3]{0:T(128)}, u32[]{:S(2)}) copy-start(f32[3]{0:T(128)} %constant.109) | copy-start | bytes 40
  171.3 97.1 %copy-start.5 = (f32[3]{0:T(128)S(1)}, f32[3]{0:T(128)}, u32[]{:S(2)}) copy-start(f32[3]{0:T(128)} %constant.106) | copy-start | bytes 40
  184.2 84.9 %collective-permute-start.3 = (f32[1]{0:T(128)}, f32[1]{0:T(128)}, u32[]{:S(2)}, u32[]{:S(2)}) collective-permute-start(f32[1]{0:T(128)} %bitcast.39), channel_id=1, source_target_pairs={{0,12},{4,0},{8,4},{12,8},{1,13},{5,1},{9,5},{13,9},{2,14},{6,2},{... | collective-permute-start | bytes 20 | tf_op jit(solution)/shard_map/ppermute | solution.py:15
where the time goes:
time: 271 us; the launch traced here: 270 us
  blocking collectives  81.3 us (30%)
  waiting for transfers between devices  67.3 us (25%)
  other arithmetic  45.3 us (17%)
  local copies, waits for them, and re-layouts  40.7 us (15%)
  matrix products  24.4 us (9%)
  starting transfers between devices  5.71 us (2%)
  between operations  5.46 us (2%)
    psum x5, blocking collectives, one_axis_at_a_time(): array = lax.psum(array, axis)  81.3 us
    ppermute x4, waiting for transfers between devices, passed_along(): return lax.ppermute(value, axis, pairs)  67.3 us
    gather x6, local copies, waits for them, and re-layouts, pair_measure(): phases = jnp.arctan2(jnp.diagonal(imag_part), jnp.diagonal(real_part))  27.1 us
    dot_general x3, matrix products, pair_measure(): lax.dot_general(left_side, right_side, (((1,), (1,)), ((), ())), preferre...  24.4 us
    select_n x2, other arithmetic, shards(): jnp.where(z_wrap, jnp.roll(z_later, -shifts[2], axis=-1), z_later)  15.8 us
    select_n x2, other arithmetic, shards(): jnp.where(y_wrap, jnp.roll(own_planes, -shifts[1], axis=-1), own_planes)  10.7 us
    transpose x3, local copies, waits for them, and re-layouts, pair_measure(): left_side = jnp.concatenate([own_point[0], own_point[1]], axis=1)  9 us
    reduce_sum x3, other arithmetic, pair_measure(): coherence = jnp.sum(real_part * real_part + imag_part * imag_part) / bands  7.5 us
  transfers between devices with their start and end apart: 4, of which 1 were waited for; matrix products, arithmetic and copies ran while one was open for 30% of the time, Pallas kernels for 0%

commit v1 on v0

--- a/solution.py
+++ b/solution.py
@@ -17,7 +17,7 @@
 
 def one_axis_at_a_time(array, axes):
     for axis in axes:
-        array = lax.psum(array, axis)
+        array = jnp.sum(lax.all_gather(array, axis), axis=0)
     return array
 
 

time: 271 us -> 306 us (1.13); the launches traced: 270 us -> 302 us
  blocking collectives: 81.3 us -> 113 us
    all_gather x0 -> x10, blocking collectives: none -> 113 us  [one_axis_at_a_time(): array = jnp.sum(lax.all_gather(array, axis), axis=0)]
    psum x5 -> x0, blocking collectives: 81.3 us -> none  [one_axis_at_a_time(): array = lax.psum(array, axis)]
  transfers between devices with their start and end apart: 4 -> 4, of which waited for: 1 -> 1; matrix products, arithmetic and copies ran while one was open for 30% -> 27% of each run, Pallas kernels for 0% -> 0%
where the time goes in v1:
time: 306 us; the launch traced here: 302 us
  blocking collectives  113 us (37%)
  waiting for transfers between devices  67.3 us (22%)
  other arithmetic  45.6 us (15%)
  local copies, waits for them, and re-layouts  40.8 us (13%)
  matrix products  24.4 us (8%)
  between operations  5.5 us (2%)
  starting transfers between devices  5.01 us (2%)
    all_gather x10, blocking collectives, one_axis_at_a_time(): array = jnp.sum(lax.all_gather(array, axis), axis=0)  113 us
    ppermute x4, waiting for transfers between devices, passed_along(): return lax.ppermute(value, axis, pairs)  67.3 us
    gather x6, local copies, waits for them, and re-layouts, pair_measure(): phases = jnp.arctan2(jnp.diagonal(imag_part), jnp.diagonal(real_part))  27.1 us
    dot_general x3, matrix products, pair_measure(): lax.dot_general(left_side, right_side, (((1,), (1,)), ((), ())), preferre...  24.4 us
    select_n x2, other arithmetic, shards(): jnp.where(z_wrap, jnp.roll(z_later, -shifts[2], axis=-1), z_later)  15.8 us
    select_n x2, other arithmetic, shards(): jnp.where(y_wrap, jnp.roll(own_planes, -shifts[1], axis=-1), own_planes)  10.7 us
    transpose x3, local copies, waits for them, and re-layouts, pair_measure(): left_side = jnp.concatenate([own_point[0], own_point[1]], axis=1)  9 us
    reduce_sum x3, other arithmetic, pair_measure(): coherence = jnp.sum(real_part * real_part + imag_part * imag_part) / bands  7.5 us
  transfers between devices with their start and end apart: 4, of which 1 were waited for; matrix products, arithmetic and copies ran while one was open for 27% of the time, Pallas kernels for 0%

profile of v1, /device:TPU:2, one launch (start us, length us, event | category | flops | bytes accessed | tf_op | source)
XLA Modules:
  0.0 301.5 jit_solution(8143050686592515394)
XLA Ops:
  0.6 3.1 %collective-permute-start.2 = (bf16[2,1,512,2048]{3,2,0,1:T(8,128)(2,1)}, bf16[2,1,512,2048]{3,2,0,1:T(8,128)(2,1)}, u32[]{:S(2)}, u32[]{:S(2)}) collective-permute-start(bf16[2,1,512,2048]{3,2,0,1:T(8,128)(2,1)} %bitcast.100), channel_id=1, source_target_pairs={{0,3},{1,0},{2,1},{3,2},{4,7},{5,4},{6,5},{7,6},{8,11},{9,8},{10,9... | collective-permute-start | bytes 12582920 | tf_op jit(solution)/shard_map/ppermute | solution.py:15
  8.2 6.5 %fusion.39 = bf16[2,1,512,2048]{3,2,1,0:T(8,128)(2,1)S(1)} fusion(bf16[2,1,512,2048]{3,2,0,1:T(8,128)(2,1)} %bitcast.103, s32[]{:T(128)S(6)} %select_n.67, pred[]{:T(512)S(6)} %eq.14), kind=kLoop, calls=%fused_computation.81 | loop fusion | flops 10485760 | bytes 8388613 | tf_op jit(solution)/shard_map/jit(_where)/select_n | solution.py:58
  18.3 4.2 %fusion.24 = bf16[2,1,512,2048]{3,2,0,1:T(8,128)(2,1)S(1)} fusion(bf16[2,1,512,2048]{3,2,0,1:T(8,128)(2,1)S(1)} %bitcast.104, s32[]{:T(128)S(6)} %select_n.67, pred[]{:T(512)S(6)} %eq.14), kind=kLoop, calls=%fused_computation.39 | loop fusion | flops 10485760 | bytes 8388613 | tf_op jit(solution)/shard_map/jit(_where)/select_n | solution.py:58
  24.1 2.5 slice_bitcast_fusion.7
  26.5 67.3 %collective-permute-done.2 = bf16[2,1,512,2048]{3,2,0,1:T(8,128)(2,1)} collective-permute-done((bf16[2,1,512,2048]{3,2,0,1:T(8,128)(2,1)}, bf16[2,1,512,2048]{3,2,0,1:T(8,128)(2,1)}, u32[]{:S(2)}, u32[]{:S(2)}) %collective-permute-start.2) | collective-permute-done | bytes 4194336 | tf_op jit(solution)/shard_map/ppermute | solution.py:15
  93.9 7.8 %fusion.40 = bf16[2,1,512,2048]{3,2,1,0:T(8,128)(2,1)S(1)} fusion(bf16[2,1,512,2048]{3,2,0,1:T(8,128)(2,1)} %collective-permute-done.2, s32[]{:T(128)S(6)} %select_n.69, pred[]{:T(512)S(6)} %eq.15), kind=kLoop, calls=%fused_computation.82 | loop fusion | flops 10485760 | bytes 8388613 | tf_op jit(solution)/shard_map/jit(_where)/select_n | solution.py:63
  102.0 8.0 %fusion.22 = bf16[2,1,512,2048]{3,2,0,1:T(8,128)(2,1)S(1)} fusion(bf16[2,1,512,2048]{3,2,0,1:T(8,128)(2,1)} %collective-permute-done.2, s32[]{:T(128)S(6)} %select_n.69, pred[]{:T(512)S(6)} %eq.15), kind=kLoop, calls=%fused_computation.37 | loop fusion | flops 10485760 | bytes 8388613 | tf_op jit(solution)/shard_map/jit(_where)/select_n | solution.py:63
  110.1 8.2 %fusion.29 = f32[1,512,1024]{2,1,0:T(8,128)} fusion(bf16[1,512,2048]{2,1,0:T(8,128)(2,1)S(1)} %fusion.36, bf16[1,512,2048]{2,1,0:T(8,128)(2,1)S(1)} %slice_bitcast_fusion, bf16[1,512,2048]{2,1,0:T(8,128)(2,1)S(1)} %slice_bitcast_fusion.1, bf16[1,512,2048]{2,1,0:T(8,128)(2,1)} %get-tuple-element.8, bf16[1,512,2048]{2,1,0:T(8,128)(2,1)} %get-tuple-element.7), kind=kOutput, calls=%fused_computation.54 | convolution fusion | flops 4336910336 | bytes 12582912 | tf_op jit(solution)/shard_map/vmap()/dot_general | solution.py:34
  118.3 2.5 add_reduce_fusion
  120.8 4.5 %gather_fusion.4 = f32[512]{0:T(512)S(1)} fusion(f32[512,512]{1,0:T(8,128)S(1)} %get-tuple-element.17, s32[512]{0:T(512)S(1)} %bitcast.94), kind=kCustom, calls=%fused_computation.4 | custom fusion | bytes 8192 | tf_op jit(solution)/shard_map/vmap(jit(diagonal))/cond/branch_0_fun/gather | solution.py:39
  125.3 4.5 %gather_fusion.5 = f32[512]{0:T(512)S(1)} fusion(f32[512,512]{1,0:T(8,128)S(1)} %get-tuple-element.16, s32[512]{0:T(512)S(1)} %bitcast.95), kind=kCustom, calls=%fused_computation.5 | custom fusion | bytes 8192 | tf_op jit(solution)/shard_map/vmap(jit(diagonal))/cond/branch_0_fun/gather | solution.py:39
  129.9 3.3 %slice_bitcast_fusion.5 = bf16[1,512,2048]{2,1,0:T(8,128)(2,1)} fusion(bf16[2,1,512,2048]{3,2,1,0:T(8,128)(2,1)} %bitcast.12), kind=kLoop, calls=%fused_computation.51 | loop fusion | bytes 4194304 | tf_op jit(solution)/shard_map/vmap()/squeeze;vmap()/transpose | solution.py:26
  133.2 3.2 %slice_bitcast_fusion.4 = bf16[1,512,2048]{2,1,0:T(8,128)(2,1)} fusion(bf16[2,1,512,2048]{3,2,0,1:T(8,128)(2,1)} %collective-permute-done.1), kind=kLoop, calls=%fused_computation.50 | loop fusion | bytes 4194304 | tf_op jit(solution)/shard_map/vmap()/squeeze;vmap()/transpose | solution.py:26
  136.4 8.1 %fusion.30 = f32[1,512,1024]{2,1,0:T(8,128)} fusion(bf16[1,512,2048]{2,1,0:T(8,128)(2,1)S(1)} %copy-done.1, bf16[1,512,2048]{2,1,0:T(8,128)(2,1)S(1)} %copy-done.3, bf16[1,512,2048]{2,1,0:T(8,128)(2,1)S(1)} %copy-done.2, bf16[1,512,2048]{2,1,0:T(8,128)(2,1)} %slice_bitcast_fusion.4, bf16[1,512,2048]{2,1,0:T(8,128)(2,1)} %slice_bitcast_fusion.5), kind=kOutput, calls=%fused_computation.55 | convolution fusion | flops 4336910336 | bytes 12582912 | tf_op jit(solution)/shard_map/vmap()/dot_general | solution.py:34
  144.5 2.5 add_reduce_fusion.1
  147.0 4.5 %gather_fusion.2 = f32[512]{0:T(512)S(1)} fusion(f32[512,512]{1,0:T(8,128)S(1)} %get-tuple-element.14, s32[512]{0:T(512)S(1)} %bitcast.96), kind=kCustom, calls=%fused_computation.2 | custom fusion | bytes 8192 | tf_op jit(solution)/shard_map/vmap(jit(diagonal))/cond/branch_0_fun/gather | solution.py:39
  151.5 4.5 %gather_fusion.3 = f32[512]{0:T(512)S(1)} fusion(f32[512,512]{1,0:T(8,128)S(1)} %get-tuple-element.13, s32[512]{0:T(512)S(1)} %bitcast.97), kind=kCustom, calls=%fused_computation.3 | custom fusion | bytes 8192 | tf_op jit(solution)/shard_map/vmap(jit(diagonal))/cond/branch_0_fun/gather | solution.py:39
  156.1 6.7 %fusion.26 = bf16[2,512,2048]{2,1,0:T(8,128)(2,1)S(1)} fusion(bf16[2,512,2048]{2,1,0:T(8,128)(2,1)} %collective-permute-done, s32[]{:T(128)S(6)} %select_n.58, pred[]{:T(512)S(6)} %eq.13), kind=kLoop, calls=%fused_computation.41 | loop fusion | flops 10485760 | bytes 8388613 | tf_op jit(solution)/shard_map/jit(_where)/select_n | solution.py:53
  163.2 8.1 %fusion.31 = f32[1,512,1024]{2,1,0:T(8,128)} fusion(bf16[1,512,2048]{2,1,0:T(8,128)(2,1)S(1)} %get-tuple-element.5, bf16[1,512,2048]{2,1,0:T(8,128)(2,1)S(1)} %get-tuple-element.6, bf16[1,512,2048]{2,1,0:T(8,128)(2,1)S(1)} %get-tuple-element.4, bf16[1,512,2048]{2,1,0:T(8,128)(2,1)} %get-tuple-element.8, bf16[1,512,2048]{2,1,0:T(8,128)(2,1)} %get-tuple-element.7), kind=kOutput, calls=%fused_computation.56 | convolution fusion | flops 4336910336 | bytes 12582912 | tf_op jit(solution)/shard_map/vmap()/dot_general | solution.py:34
  171.3 2.5 add_reduce_fusion.2
  173.8 4.5 %gather_fusion = f32[512]{0:T(512)S(1)} fusion(f32[512,512]{1,0:T(8,128)S(1)} %get-tuple-element.11, s32[512]{0:T(512)S(1)} %bitcast.98), kind=kCustom, calls=%fused_computation | custom fusion | bytes 8192 | tf_op jit(solution)/shard_map/vmap(jit(diagonal))/cond/branch_0_fun/gather | solution.py:39
  178.4 4.5 %gather_fusion.1 = f32[512]{0:T(512)S(1)} fusion(f32[512,512]{1,0:T(8,128)S(1)} %get-tuple-element.10, s32[512]{0:T(512)S(1)} %bitcast.99), kind=kCustom, calls=%fused_computation.1 | custom fusion | bytes 8192 | tf_op jit(solution)/shard_map/vmap(jit(diagonal))/cond/branch_0_fun/gather | solution.py:39
  183.0 28.5 %all-gather = f32[24,1,512]{2,1,0:T(1,128)S(1)} all-gather(f32[3,1,512]{2,1,0:T(1,128)S(1)} %pad_maximum_fusion), channel_id=2, replica_groups=mesh['kx_0'=8,'kx_1'=2,'ky_0'=2,'ky_1'=2,'kz'=4] {'kx_0'}, dimensions={0}, use_global_device_ids=true | all-gather | bytes 55296 | tf_op jit(solution)/shard_map/all_gather | solution.py:20
  211.7 16.3 %all-gather.9 = f32[2,3,512]{2,1,0:T(4,128)S(1)} all-gather(f32[1,3,512]{2,1,0:T(4,128)S(1)} %bitcast.105), channel_id=3, replica_groups=mesh['kx_0'=8,'kx_1'=2,'ky_0'=2,'ky_1'=2,'kz'=4] {'kx_1'}, dimensions={0}, use_global_device_ids=true | all-gather | bytes 18432 | tf_op jit(solution)/shard_map/all_gather | solution.py:20
  228.0 5.9 %all-gather.10 = f32[2,3,512]{2,1,0:T(4,128)S(1)} all-gather(f32[1,3,512]{2,1,0:T(4,128)S(1)} %bitcast.106), channel_id=4, replica_groups=mesh['kx_0'=8,'kx_1'=2,'ky_0'=2,'ky_1'=2,'kz'=4] {'ky_0'}, dimensions={0}, use_global_device_ids=true | all-gather | bytes 18432 | tf_op jit(solution)/shard_map/all_gather | solution.py:20
  233.9 1.8 all-gather.11
  235.7 11.9 %all-gather.12 = f32[4,3,512]{2,1,0:T(4,128)S(1)} all-gather(f32[1,3,512]{2,1,0:T(4,128)S(1)} %bitcast.108), channel_id=6, replica_groups=mesh['kx_0'=8,'kx_1'=2,'ky_0'=2,'ky_1'=2,'kz'=4] {'kz'}, dimensions={0}, use_global_device_ids=true | all-gather | bytes 30720 | tf_op jit(solution)/shard_map/all_gather | solution.py:20
  247.7 24.6 %all_gather.68 = f32[8,3,512]{2,1,0:T(4,128)S(1)} all-gather(f32[1,3,512]{2,1,0:T(4,128)S(1)} %maximum_multiply_fusion), channel_id=1, replica_groups=mesh['kx_0'=8,'kx_1'=2,'ky_0'=2,'ky_1'=2,'kz'=4] {'kx_0'}, dimensions={0}, use_global_device_ids=true | all-gather | bytes 55296 | tf_op jit(solution)/shard_map/all_gather | solution.py:20
  272.3 4.4 %all-gather.13 = f32[2,3,512]{2,1,0:T(4,128)S(1)} all-gather(f32[1,3,512]{2,1,0:T(4,128)S(1)} %bitcast.109), channel_id=7, replica_groups=mesh['kx_0'=8,'kx_1'=2,'ky_0'=2,'ky_1'=2,'kz'=4] {'kx_1'}, dimensions={0}, use_global_device_ids=true | all-gather | bytes 18432 | tf_op jit(solution)/shard_map/all_gather | solution.py:20
  276.7 5.9 %all-gather.14 = f32[2,3,512]{2,1,0:T(4,128)S(1)} all-gather(f32[1,3,512]{2,1,0:T(4,128)S(1)} %bitcast.110), channel_id=8, replica_groups=mesh['kx_0'=8,'kx_1'=2,'ky_0'=2,'ky_1'=2,'kz'=4] {'ky_0'}, dimensions={0}, use_global_device_ids=true | all-gather | bytes 18432 | tf_op jit(solution)/shard_map/all_gather | solution.py:20
  282.6 1.8 all-gather.15
  284.4 11.9 %all-gather.16 = f32[4,3,512]{2,1,0:T(4,128)S(1)} all-gather(f32[1,3,512]{2,1,0:T(4,128)S(1)} %bitcast.112), channel_id=10, replica_groups=mesh['kx_0'=8,'kx_1'=2,'ky_0'=2,'ky_1'=2,'kz'=4] {'kz'}, dimensions={0}, use_global_device_ids=true | all-gather | bytes 30720 | tf_op jit(solution)/shard_map/all_gather | solution.py:20
  (47 shorter events, 11.4 us)
Async XLA Ops:
  0.6 93.2 %collective-permute-start.2 = (bf16[2,1,512,2048]{3,2,0,1:T(8,128)(2,1)}, bf16[2,1,512,2048]{3,2,0,1:T(8,128)(2,1)}, u32[]{:S(2)}, u32[]{:S(2)}) collective-permute-start(bf16[2,1,512,2048]{3,2,0,1:T(8,128)(2,1)} %bitcast.100), channel_id=1, source_target_pairs={{0,3},{1,0},{2,1},{3,2},{4,7},{5,4},{6,5},{7,6},{8,11},{9,8},{10,9... | collective-permute-start | bytes 12582920 | tf_op jit(solution)/shard_map/ppermute | solution.py:15
  3.7 126.1 %collective-permute-start.1 = (bf16[2,1,512,2048]{3,2,0,1:T(8,128)(2,1)}, bf16[2,1,512,2048]{3,2,0,1:T(8,128)(2,1)}, u32[]{:S(2)}, u32[]{:S(2)}) collective-permute-start(bf16[2,1,512,2048]{3,2,0,1:T(8,128)(2,1)} %bitcast.101), channel_id=1, source_target_pairs={{0,4},{4,8},{8,12},{12,0},{1,5},{5,9},{9,13},{13,1},{2,6},{6,10},{... | collective-permute-start | bytes 12582920 | tf_op jit(solution)/shard_map/ppermute | solution.py:15
  3.7 152.3 %collective-permute-start = (bf16[2,512,2048]{2,1,0:T(8,128)(2,1)}, bf16[2,512,2048]{2,1,0:T(8,128)(2,1)}, u32[]{:S(2)}, u32[]{:S(2)}) collective-permute-start(bf16[2,512,2048]{2,1,0:T(8,128)(2,1)} %bitcast.102), channel_id=1, source_target_pairs={{0,240},{16,0},{32,16},{48,32},{64,48},{80,64},{96,80},{112,96},{1... | collective-permute-start | bytes 12582920 | tf_op jit(solution)/shard_map/ppermute | solution.py:15
  14.7 3.6 %copy-start = (bf16[2,1,1,1,512,2048]{5,4,3,2,1,0:T(8,128)(2,1)S(1)}, bf16[2,1,1,1,512,2048]{5,4,3,2,1,0:T(8,128)(2,1)}, u32[]{:S(2)}) copy-start(bf16[2,1,1,1,512,2048]{5,4,3,2,1,0:T(8,128)(2,1)} %param.5) | copy-start | bytes 12582916
  129.9 6.6 %copy-start.1 = (bf16[1,512,2048]{2,1,0:T(8,128)(2,1)S(1)}, bf16[1,512,2048]{2,1,0:T(8,128)(2,1)}, u32[]{:S(2)}) copy-start(bf16[1,512,2048]{2,1,0:T(8,128)(2,1)} %fusion.35) | copy-start | bytes 6291460
  129.9 6.5 %copy-start.2 = (bf16[1,512,2048]{2,1,0:T(8,128)(2,1)S(1)}, bf16[1,512,2048]{2,1,0:T(8,128)(2,1)}, u32[]{:S(2)}) copy-start(bf16[1,512,2048]{2,1,0:T(8,128)(2,1)} %slice_bitcast_fusion.3) | copy-start | bytes 6291460
  129.9 6.5 %copy-start.3 = (bf16[1,512,2048]{2,1,0:T(8,128)(2,1)S(1)}, bf16[1,512,2048]{2,1,0:T(8,128)(2,1)}, u32[]{:S(2)}) copy-start(bf16[1,512,2048]{2,1,0:T(8,128)(2,1)} %slice_bitcast_fusion.2) | copy-start | bytes 6291460
  171.3 128.3 %copy-start.4 = (f32[3]{0:T(128)S(1)}, f32[3]{0:T(128)}, u32[]{:S(2)}) copy-start(f32[3]{0:T(128)} %constant.109) | copy-start | bytes 40
  171.3 128.4 %copy-start.5 = (f32[3]{0:T(128)S(1)}, f32[3]{0:T(128)}, u32[]{:S(2)}) copy-start(f32[3]{0:T(128)} %constant.106) | copy-start | bytes 40
  297.6 2.7 collective-permute-start.3
